TPU v7x, 32 devices: a whole 2x2x4 slice. The times are simulated.
32 devices in a mesh: lat: 8 (over z, y), lon: 4 (over x, core).
Axes of the slice: x: 2, y: 2, z: 4, core: 2. Of those that a mesh axis runs over, the one named last changes fastest.
Arguments:
- field: bfloat16 [150, 128, 1024], P(None, 'lat', 'lon'), may hold values from -6 to 6
- land_mask: int32 [128, 1024], P('lat', 'lon'), may hold values 0 or 1
- fold_partner: int32 [1024], replicated, may hold values from 0 to 1023, as said below
- dw_kernel: float32 [150, 7, 7], replicated, may hold values from -0.875 to 0.875
- norm_gain: float32 [150], replicated, may hold values from 0.1 to 1.9
- w_in: bfloat16 [150, 600], replicated, may hold values from -0.5 to 0.5
- w_out: bfloat16 [600, 150], replicated, may hold values from -0.25 to 0.25
- spec_gain: float32 [2, 150, 512], replicated, may hold values from -12 to 12
- mix_weight: bfloat16 [150, 150], replicated, may hold values from -0.5 to 0.5
Outputs:
- block_out: bfloat16 [150, 128, 1024], P(None, 'lat', 'lon')
Inputs may be any that keep to these rules, and one draw needn't show every extreme that they name: There is one s such that fold_partner[j] = (s - j) mod 1024 for every j.
All inputs are finite; a program needn't handle non-finite values. No bound on the sum of `land_mask` on one device may be relied on, other than what follows from the above.
Results may differ from a plain program's by a relative error of at most 0.0065.
Values may be sent and summed in bfloat16 or wider, within the bound.
A program may use at most 128 MiB of HBM per device.

v0:
```python
import math

import jax
import jax.numpy as jnp
from jax import lax
from jax.sharding import PartitionSpec as P


def extended_2(cells, sides, width, closed):
    for axis, dim in sides:
        count = lax.axis_size(axis)
        ends = count if closed else count - 1
        head = lax.slice_in_dim(cells, 0, width, axis=dim)
        tail = lax.slice_in_dim(cells, cells.shape[dim] - width, cells.shape[dim], axis=dim)
        cells = jnp.concatenate(
            [
                lax.ppermute(tail, axis, [(i, (i + 1) % count) for i in range(ends)]),
                cells,
                lax.ppermute(head, axis, [((i + 1) % count, i) for i in range(ends)]),
            ],
            axis=dim,
        )
    return cells


def dft_table(lon_points, mode_count, col_count):
    points = jnp.arange(col_count, dtype=jnp.int32)
    freqs = jnp.arange(mode_count, dtype=jnp.int32)
    phase_index = points[:, None] * freqs[None, :] % lon_points
    angles = phase_index.astype(jnp.float32) * (2.0 * math.pi / lon_points)
    factor = 1.0 / math.sqrt(lon_points)
    return jnp.concatenate([jnp.cos(angles) * factor, -jnp.sin(angles) * factor], axis=1).astype(
        jnp.bfloat16
    )


def apply_gain(spectrum, spec_gain, mode_count):
    spec_re = spectrum[..., :mode_count]
    spec_im = spectrum[..., mode_count:]
    gain_re = spec_gain[0][:, None, :]
    gain_im = spec_gain[1][:, None, :]
    return jnp.concatenate(
        [gain_re * spec_re - gain_im * spec_im, gain_re * spec_im + gain_im * spec_re], axis=-1
    ).astype(jnp.bfloat16)


def depthwise_conv(extended, dw_kernel, lat_rows, lon_cols):
    total = jnp.zeros((extended.shape[0], lat_rows, lon_cols), jnp.float32)
    for tap_row in range(7):
        for tap_col in range(7):
            weight_col = dw_kernel[:, tap_row, tap_col][:, None, None]
            total = total + weight_col * extended[
                :, tap_row : tap_row + lat_rows, tap_col : tap_col + lon_cols
            ].astype(jnp.float32)
    return total


def point_mixer(depth, masked, wet_grid, norm_gain, w_in, w_out):
    channels = depth.shape[0]
    flat = depth.reshape(channels, -1)
    average = jnp.mean(flat, axis=0, keepdims=True)
    centred = flat - average
    variance = jnp.mean(centred * centred, axis=0, keepdims=True)
    normed = (centred * lax.rsqrt(variance + 1e-06) * norm_gain[:, None]).astype(jnp.bfloat16)
    pre_act = jnp.einsum("ch,cp->hp", w_in, normed, preferred_element_type=jnp.float32)
    hidden = jax.nn.gelu(pre_act, approximate=True).astype(jnp.bfloat16)
    branch = jnp.einsum("hc,hp->cp", w_out, hidden, preferred_element_type=jnp.float32)
    wet_flat = wet_grid.reshape(1, -1).astype(jnp.float32)
    result = wet_flat * (masked.reshape(channels, -1).astype(jnp.float32) + branch)
    return result.astype(jnp.bfloat16).reshape(depth.shape)


def local(field, land_mask, fold_partner, dw_kernel, norm_gain, w_in, w_out, spec_gain, mix_weight):
    channels, lat_rows, lon_cols = field.shape
    lat_count = lax.axis_size("lat")
    lon_count = lax.axis_size("lon")
    lon_points = lon_cols * lon_count
    mode_count = spec_gain.shape[2]
    wet_grid = land_mask.astype(field.dtype)
    masked = field * wet_grid[None]
    top_rows = masked[:, lat_rows - 3 :, :][:, ::-1, :]
    fold_full = lax.all_gather(top_rows, "lon", axis=2, tiled=True)
    lon_first = lax.axis_index("lon") * lon_cols
    window = (lon_first - 3 + jnp.arange(lon_cols + 6, dtype=jnp.int32)) % lon_points
    ghost_rows = jnp.take(fold_full, jnp.take(fold_partner, window), axis=2)
    lat_index = lax.axis_index("lat")
    lon_padded = extended_2(masked, (("lon", 2),), 3, True)
    padded = extended_2(lon_padded, (("lat", 1),), 3, False)
    south_rows = padded[:, :3]
    north_rows = jnp.where(lat_index == lat_count - 1, ghost_rows, padded[:, lat_rows + 3 :])
    extended = jnp.concatenate([south_rows, padded[:, 3 : lat_rows + 3], north_rows], axis=1)
    depth = depthwise_conv(extended, dw_kernel, lat_rows, lon_cols)
    group_rows = math.gcd(lat_rows, 8)

    def mix_rows(group_index, result):
        offset = group_index * group_rows
        mixed_block = point_mixer(
            lax.dynamic_slice_in_dim(depth, offset, group_rows, 1),
            lax.dynamic_slice_in_dim(masked, offset, group_rows, 1),
            lax.dynamic_slice_in_dim(wet_grid, offset, group_rows, 0),
            norm_gain,
            w_in,
            w_out,
        )
        return lax.dynamic_update_slice_in_dim(result, mixed_block, offset, 1)

    residual = lax.fori_loop(
        0, lat_rows // group_rows, mix_rows, jnp.zeros(field.shape, jnp.bfloat16)
    )
    by_rows = lax.all_to_all(residual, "lon", split_axis=1, concat_axis=2, tiled=True)
    row_count = by_rows.shape[1]
    fourier = dft_table(lon_points, mode_count, lon_points)
    spectrum = jnp.dot(
        by_rows.reshape(channels * row_count, lon_points),
        fourier,
        preferred_element_type=jnp.float32,
    )
    scaled = apply_gain(
        spectrum.reshape(channels, row_count, 2 * mode_count), spec_gain, mode_count
    )
    along_rows = jnp.einsum(
        "crk,nk->crn", scaled, fourier, preferred_element_type=jnp.float32
    ).astype(jnp.bfloat16)
    spatial = lax.all_to_all(along_rows, "lon", split_axis=2, concat_axis=1, tiled=True)
    mixed = jnp.einsum(
        "cd,cp->dp", mix_weight, spatial.reshape(channels, -1), preferred_element_type=jnp.float32
    )
    wet_flat = wet_grid.reshape(1, -1).astype(jnp.float32)
    output = wet_flat * (residual.reshape(channels, -1).astype(jnp.float32) + mixed)
    return output.astype(jnp.bfloat16).reshape(field.shape)


def solution(mesh):
    placed = (P(None, "lat", "lon"), P("lat", "lon"), P(), P(), P(), P(), P(), P(), P())
    return jax.shard_map(
        local, mesh=mesh, in_specs=placed, out_specs=P(None, "lat", "lon"), check_vma=False
    )
```

profile of v0, /device:TPU:0, one launch (start us, length us, event | category | flops | bytes accessed | tf_op | source)
XLA Modules:
  0.0 203.4 jit_solution(11672251696216430919)
XLA Ops:
  0.9 4.5 %copy.33 = bf16[150,16,256]{0,1,2:T(8,128)(2,1)} copy(bf16[150,16,256]{2,1,0:T(8,128)(2,1)} %param.11) | data formatting | bytes 2457600 | tf_op args[0]
  5.4 1.9 broadcast_multiply_fusion.1
  8.4 1.9 collective-permute-start.1
  12.0 1.2 rev.3
  13.4 10.2 %all_gather.3 = bf16[150,3,1024]{2,0,1:T(8,128)(2,1)S(1)} all-gather(bf16[150,3,256]{2,0,1:T(8,128)(2,1)S(1)} %copy.36), channel_id=1, replica_groups=mesh['lat'=8,'lon'=4] {'lon'}, dimensions={2}, use_global_device_ids=true | all-gather | bytes 1152000 | tf_op jit(solution)/shard_map/all_gather | solution.py:82
  23.7 1.7 gather_fusion
  26.0 1.5 pad_maximum_fusion.5
  27.4 1.4 copy.38
  28.8 1.3 collective-permute-start.3
  30.1 3.2 %copy.40 = bf16[150,16,256]{2,1,0:T(8,128)(2,1)} copy(bf16[150,16,256]{0,1,2:T(8,128)(2,1)S(1)} %broadcast_multiply_fusion.1) | data formatting | bytes 2457600 | tf_op jit(solution)/shard_map/while | solution.py:107
  33.3 2.5 %copy.37 = bf16[150,3,1024]{0,1,2:T(4,128)(2,1)} copy(bf16[150,3,1024]{2,0,1:T(8,128)(2,1)S(1)} %all_gather.3) | data formatting | bytes 1843200 | tf_op jit(solution)/shard_map/all_gather | solution.py:82
  35.8 3.6 %gather_fusion.1 = bf16[262,150,3]{1,2,0:T(4,128)(2,1)} fusion(bf16[150,3,1024]{0,1,2:T(4,128)(2,1)} %copy.37, s32[1024]{0:T(1024)S(1)} %pad_clamp_fusion), kind=kCustom, calls=%fused_computation.1 | custom fusion | bytes 472648 | tf_op jit(solution)/shard_map/jit(_take)/gather | solution.py:85
  39.5 1.6 fusion.48
  41.1 2.1 %copy.34 = bf16[150,3,262]{2,0,1:T(8,128)(2,1)} copy(bf16[150,3,262]{0,1,2:T(4,128)(2,1)} %get-tuple-element.195) | data formatting | bytes 471600 | tf_op jit(solution)/shard_map/slice | solution.py:14
  43.2 5.3 %collective-permute-start.2 = (bf16[150,3,262]{2,0,1:T(8,128)(2,1)}, bf16[150,3,262]{2,0,1:T(8,128)(2,1)}, u32[]{:S(2)}, u32[]{:S(2)}) collective-permute-start(bf16[150,3,262]{2,0,1:T(8,128)(2,1)} %copy.34), channel_id=1, source_target_pairs={{0,4},{4,8},{8,12},{12,16},{16,20},{20,24},{24,28},{1,5},{5,9},{9,... | collective-permute-start | bytes 707408 | tf_op jit(solution)/shard_map/ppermute | solution.py:17
  48.5 1.3 copy.39
  49.8 2.0 bitcast_select_fusion
  51.8 3.9 %collective-permute-done.2 = bf16[150,3,262]{2,0,1:T(8,128)(2,1)} collective-permute-done((bf16[150,3,262]{2,0,1:T(8,128)(2,1)}, bf16[150,3,262]{2,0,1:T(8,128)(2,1)}, u32[]{:S(2)}, u32[]{:S(2)}) %collective-permute-start.2) | collective-permute-done | bytes 235832 | tf_op jit(solution)/shard_map/ppermute | solution.py:17
  55.7 1.3 copy.35
  57.4 5.1 %maximum_maximum_fusion = (bf16[150,19,262]{0,1,2:T(8,128)(2,1)S(1)}, bf16[150,19,262]{0,1,2:T(8,128)(2,1)S(1)}) fusion(bf16[150,16,3]{0,1,2:T(8,128)(2,1)S(1)} %collective-permute-done.1, bf16[150,16,256]{0,1,2:T(8,128)(2,1)S(1)} %broadcast_multiply_fusion.1, bf16[150,16,3]{0,1,2:T(8,128)(2,1)S(1)} %collective-permute-done, ...), kind=kLoop, calls=%fused_computation.36 | loop fusion | flops 11947200 | bytes 4716000 | tf_op jit(solution)/shard_map/concatenate | solution.py:91
  63.0 41.2 %multiply_add_fusion = f32[150,16,256]{0,1,2:T(8,128)} fusion(bf16[150,16,256]{0,1,2:T(8,128)(2,1)S(1)} %broadcast_multiply_fusion.1, bf16[150,16,3]{0,1,2:T(8,128)(2,1)S(1)} %collective-permute-done.1, bf16[150,16,3]{0,1,2:T(8,128)(2,1)S(1)} %collective-permute-done, bf16[150,19,262]{0,1,2:T(8,128)(2,1)S(1)} %get-tuple-element.194, ...), kind=kLoop, calls=%fused_computation.35 | loop fusion | flops 93388800 | bytes 55354200 | tf_op jit(solution)/shard_map/add | solution.py:52
  104.2 5.2 %copy.41 = f32[150,16,256]{2,1,0:T(8,128)} copy(f32[150,16,256]{0,1,2:T(8,128)} %multiply_add_fusion) | data formatting | bytes 4915200 | tf_op jit(solution)/shard_map/while | solution.py:107
  109.3 1.1 broadcast_in_dim.33
  110.5 16.3 %while.13 = (s32[]{:T(128)}, bf16[150,16,256]{2,1,0:T(8,128)(2,1)}, bf16[16,256]{1,0:T(8,128)(2,1)S(1)}, bf16[150,16,256]{2,1,0:T(8,128)(2,1)}, f32[150,16,256]{...) while((s32[]{:T(128)}, bf16[150,16,256]{2,1,0:T(8,128)(2,1)}, ...), condition=%wide.region_3.4_spmd, body=%wide.region_0.3_spmd.sunk | while | flops 752029696 | bytes 21516636 | solution.py:107
  110.5 1.5 fusion.63
  112.7 1.2 dynamic-slice_convert_fusion.2
  114.5 3.1 %fusion.65 = bf16[150,2048]{1,0:T(8,128)(2,1)S(1)} fusion(f32[150,2048]{1,0:T(8,128)S(1)} %bitcast.157, bf16[600,150]{0,1:T(8,128)(2,1)} %get-tuple-element.344, bf16[150,600]{1,0:T(8,128)(2,1)S(1)} %get-tuple-element.343, f32[150,2048]{1,0:T(8,128)S(1)} %bitcast.156, f32[150]{0:T(256)S(1)} %get-tuple-element.342, f32[2048]{0:T(1024)S(1)} %bitcast.165, ...), kind=kOutput, calls=%fused_computation.14.clone.1 | convolution fusion | flops 750489600 | bytes 3457176 | tf_op jit(solution)/shard_map/while/body/eval_jaxpr/hc,hp->cp/dot_general | solution.py:67
  117.8 0.9 slice_dynamic-update-slice_fusion.2
  118.6 1.5 fusion.63
  120.9 1.2 dynamic-slice_convert_fusion.2
  122.6 3.1 %fusion.65 = bf16[150,2048]{1,0:T(8,128)(2,1)S(1)} fusion(f32[150,2048]{1,0:T(8,128)S(1)} %bitcast.157, bf16[600,150]{0,1:T(8,128)(2,1)} %get-tuple-element.344, bf16[150,600]{1,0:T(8,128)(2,1)S(1)} %get-tuple-element.343, f32[150,2048]{1,0:T(8,128)S(1)} %bitcast.156, f32[150]{0:T(256)S(1)} %get-tuple-element.342, f32[2048]{0:T(1024)S(1)} %bitcast.165, ...), kind=kOutput, calls=%fused_computation.14.clone.1 | convolution fusion | flops 750489600 | bytes 3457176 | tf_op jit(solution)/shard_map/while/body/eval_jaxpr/hc,hp->cp/dot_general | solution.py:67
  125.9 0.9 slice_dynamic-update-slice_fusion.2
  126.8 2.8 %copy.43 = bf16[150,16,256]{2,0,1:T(8,128)(2,1)} copy(bf16[150,16,256]{2,1,0:T(8,128)(2,1)} %get-tuple-element.144) | data formatting | bytes 2457600 | tf_op jit(solution)/shard_map/while | solution.py:107
  129.6 3.8 %all-to-all-start = ((bf16[150,16,256]{2,0,1:T(8,128)(2,1)}), bf16[150,16,256]{2,0,1:T(8,128)(2,1)S(1)}, u32[]{:S(2)}, u32[]{:S(2)}) async-start(bf16[150,16,256]{2,0,1:T(8,128)(2,1)} %copy.43), calls=%async_computation | async-start | bytes 2490368 | tf_op jit(solution)/shard_map/all_to_all | solution.py:110
  133.9 9.3 %multiply_convert_fusion.3 = (bf16[1024,512]{1,0:T(8,128)(2,1)}, bf16[1024,512]{1,0:T(8,128)(2,1)}) fusion(), kind=kLoop, calls=%fused_computation.55 | loop fusion | flops 9961472 | bytes 2097152 | tf_op jit(solution)/shard_map/convert.7
  143.3 6.4 %all-to-all-done = bf16[150,16,256]{2,0,1:T(8,128)(2,1)S(1)} async-done(((bf16[150,16,256]{2,0,1:T(8,128)(2,1)}), bf16[150,16,256]{2,0,1:T(8,128)(2,1)S(1)}, u32[]{:S(2)}, u32[]{:S(2)}) %all-to-all-start) | async-done | bytes 1228832 | tf_op jit(solution)/shard_map/all_to_all | solution.py:110
  149.7 1.0 copy.65
  150.6 0.8 dot_general.27
  151.4 3.0 %fusion.35 = f32[150,4,1024]{2,0,1:T(8,128)S(1)} fusion(bf16[150,4,1024]{2,0,1:T(8,128)(2,1)S(1)} %dot_general.27, bf16[1024,512]{1,0:T(8,128)(2,1)} %get-tuple-element.250, bf16[1024,512]{1,0:T(8,128)(2,1)} %get-tuple-element.251), kind=kOutput, calls=%fused_computation.61 | convolution fusion | flops 1262485504 | bytes 5783552 | tf_op jit(solution)/shard_map/dot_general | solution.py:113
  156.0 1.5 convolution_convert_fusion
  157.5 2.5 %copy.46 = bf16[150,4,1024]{0,1,2:T(4,128)(2,1)} copy(bf16[150,4,1024]{2,0,1:T(8,128)(2,1)S(1)} %convolution_convert_fusion) | data formatting | bytes 2457600 | tf_op jit(solution)/shard_map/convert_element_type | solution.py:123
  160.0 4.5 %all-to-all-start.1 = ((bf16[150,4,1024]{0,1,2:T(4,128)(2,1)}), bf16[150,4,1024]{0,1,2:T(4,128)(2,1)}, u32[]{:S(2)}, u32[]{:S(2)}) async-start(bf16[150,4,1024]{0,1,2:T(4,128)(2,1)} %copy.46), calls=%async_computation.1 | async-start | bytes 4194304 | tf_op jit(solution)/shard_map/all_to_all | solution.py:124
  164.8 2.0 %copy.60 = f32[19,8,16,256]{3,1,2,0:T(8,128)S(1)} copy(f32[19,8,16,256]{3,2,1,0:T(8,128)S(1)} %bitcast.160) | data formatting | bytes 4980736
  166.9 23.3 %all-to-all-done.1 = bf16[150,4,1024]{0,1,2:T(4,128)(2,1)} async-done(((bf16[150,4,1024]{0,1,2:T(4,128)(2,1)}), bf16[150,4,1024]{0,1,2:T(4,128)(2,1)}, u32[]{:S(2)}, u32[]{:S(2)}) %all-to-all-start.1) | async-done | bytes 1228832 | tf_op jit(solution)/shard_map/all_to_all | solution.py:124
  190.2 6.3 %copy.48 = bf16[150,4,4,256]{3,2,1,0:T(4,128)(2,1)} copy(bf16[150,4,4,256]{0,2,3,1:T(4,128)(2,1)} %bitcast.59) | data formatting | bytes 2457600 | tf_op jit(solution)/shard_map/all_to_all | solution.py:124
  196.5 3.5 %reshape.188 = bf16[150,4096]{1,0:T(8,128)(2,1)} reshape(bf16[150,4,4,256]{3,2,1,0:T(4,128)(2,1)} %copy.48) | data formatting | bytes 2457600 | tf_op jit(solution)/shard_map/reshape | solution.py:126
  200.1 1.9 fusion.24
  202.3 1.1 slice.532
  (144 shorter events, 10.2 us)
Async XLA Ops:
  0.0 200.1 %copy-start = (bf16[150,150]{1,0:T(8,128)(2,1)S(1)}, bf16[150,150]{1,0:T(8,128)(2,1)}, u32[]{:S(2)}) copy-start(bf16[150,150]{1,0:T(8,128)(2,1)} %param.19) | copy-start | bytes 135004
  0.9 9.8 %copy-start.6 = (f32[150,7,7]{0,2,1:T(8,128)S(1)}, f32[150,7,7]{0,2,1:T(8,128)}, u32[]{:S(2)}) copy-start(f32[150,7,7]{0,2,1:T(8,128)} %param.14) | copy-start | bytes 88204
  5.4 18.3 %copy-start.1 = (s32[1024]{0:T(1024)S(1)}, s32[1024]{0:T(1024)}, u32[]{:S(2)}) copy-start(s32[1024]{0:T(1024)} %param.13) | copy-start | bytes 12292
  8.0 18.0 %collective-permute-start = (bf16[150,16,3]{0,1,2:T(8,128)(2,1)}, bf16[150,16,3]{0,1,2:T(8,128)(2,1)S(1)}, u32[]{:S(2)}, u32[]{:S(2)}) collective-permute-start(bf16[150,16,3]{0,1,2:T(8,128)(2,1)} %get-tuple-element.197), channel_id=1, source_target_pairs={{0,1},{1,2},{2,3},{3,0},{4,5},{5,6},{6,7},{7,4},{8,9},{9,10},{10,1... | collective-permute-start | bytes 43208 | tf_op jit(solution)/shard_map/ppermute | solution.py:17
  8.4 17.5 %collective-permute-start.1 = (bf16[150,16,3]{0,1,2:T(8,128)(2,1)}, bf16[150,16,3]{0,1,2:T(8,128)(2,1)S(1)}, u32[]{:S(2)}, u32[]{:S(2)}) collective-permute-start(bf16[150,16,3]{0,1,2:T(8,128)(2,1)} %get-tuple-element.198), channel_id=1, source_target_pairs={{1,0},{2,1},{3,2},{0,3},{5,4},{6,5},{7,6},{4,7},{9,8},{10,9},{11,1... | collective-permute-start | bytes 43208 | tf_op jit(solution)/shard_map/ppermute | solution.py:19
  28.8 19.7 %collective-permute-start.3 = (bf16[150,3,262]{2,0,1:T(8,128)(2,1)S(1)}, bf16[150,3,262]{2,0,1:T(8,128)(2,1)}, u32[]{:S(2)}, u32[]{:S(2)}) collective-permute-start(bf16[150,3,262]{2,0,1:T(8,128)(2,1)S(1)} %copy.38), channel_id=1, source_target_pairs={{4,0},{8,4},{12,8},{16,12},{20,16},{24,20},{28,24},{5,1},{9,5},{13... | collective-permute-start | bytes 707408 | tf_op jit(solution)/shard_map/ppermute | solution.py:19
  30.1 19.7 %copy-start.46 = (pred[262]{0:T(512)(128)(4,1)S(1)}, pred[262]{0:T(512)(128)(4,1)}, u32[]{:S(2)}) copy-start(pred[262]{0:T(512)(128)(4,1)} %compare_and_fusion) | copy-start | bytes 790
  43.2 12.5 %collective-permute-start.2 = (bf16[150,3,262]{2,0,1:T(8,128)(2,1)}, bf16[150,3,262]{2,0,1:T(8,128)(2,1)}, u32[]{:S(2)}, u32[]{:S(2)}) collective-permute-start(bf16[150,3,262]{2,0,1:T(8,128)(2,1)} %copy.34), channel_id=1, source_target_pairs={{0,4},{4,8},{8,12},{12,16},{16,20},{20,24},{24,28},{1,5},{5,9},{9,... | collective-permute-start | bytes 707408 | tf_op jit(solution)/shard_map/ppermute | solution.py:17
  57.1 5.5 %copy-start.7 = (f32[150,1,1]{0,2,1:T(1,128)S(1)}, f32[150,1,1]{0,2,1:T(1,128)}, u32[]{:S(2)}) copy-start(f32[150,1,1]{0,2,1:T(1,128)} %get-tuple-element.223) | copy-start | bytes 1804
  57.1 5.5 %copy-start.8 = (f32[150,1,1]{0,2,1:T(1,128)S(1)}, f32[150,1,1]{0,2,1:T(1,128)}, u32[]{:S(2)}) copy-start(f32[150,1,1]{0,2,1:T(1,128)} %get-tuple-element.224) | copy-start | bytes 1804
  57.1 5.5 %copy-start.9 = (f32[150,1,1]{0,2,1:T(1,128)S(1)}, f32[150,1,1]{0,2,1:T(1,128)}, u32[]{:S(2)}) copy-start(f32[150,1,1]{0,2,1:T(1,128)} %get-tuple-element.225) | copy-start | bytes 1804
  57.1 5.5 %copy-start.10 = (f32[150,1,1]{0,2,1:T(1,128)S(1)}, f32[150,1,1]{0,2,1:T(1,128)}, u32[]{:S(2)}) copy-start(f32[150,1,1]{0,2,1:T(1,128)} %get-tuple-element.226) | copy-start | bytes 1804
  57.1 5.5 %copy-start.11 = (f32[150,1,1]{0,2,1:T(1,128)S(1)}, f32[150,1,1]{0,2,1:T(1,128)}, u32[]{:S(2)}) copy-start(f32[150,1,1]{0,2,1:T(1,128)} %get-tuple-element.227) | copy-start | bytes 1804
  57.1 5.5 %copy-start.12 = (f32[150,1,1]{0,2,1:T(1,128)S(1)}, f32[150,1,1]{0,2,1:T(1,128)}, u32[]{:S(2)}) copy-start(f32[150,1,1]{0,2,1:T(1,128)} %get-tuple-element.228) | copy-start | bytes 1804
  57.1 5.5 %copy-start.13 = (f32[150,1,1]{0,2,1:T(1,128)S(1)}, f32[150,1,1]{0,2,1:T(1,128)}, u32[]{:S(2)}) copy-start(f32[150,1,1]{0,2,1:T(1,128)} %get-tuple-element.229) | copy-start | bytes 1804
  57.1 5.5 %copy-start.14 = (f32[150,1,1]{0,2,1:T(1,128)S(1)}, f32[150,1,1]{0,2,1:T(1,128)}, u32[]{:S(2)}) copy-start(f32[150,1,1]{0,2,1:T(1,128)} %get-tuple-element.230) | copy-start | bytes 1804
  57.1 5.5 %copy-start.15 = (f32[150,1,1]{0,2,1:T(1,128)S(1)}, f32[150,1,1]{0,2,1:T(1,128)}, u32[]{:S(2)}) copy-start(f32[150,1,1]{0,2,1:T(1,128)} %get-tuple-element.231) | copy-start | bytes 1804
  57.1 5.5 %copy-start.16 = (f32[150,1,1]{0,2,1:T(1,128)S(1)}, f32[150,1,1]{0,2,1:T(1,128)}, u32[]{:S(2)}) copy-start(f32[150,1,1]{0,2,1:T(1,128)} %get-tuple-element.232) | copy-start | bytes 1804
  57.2 5.5 %copy-start.17 = (f32[150,1,1]{0,2,1:T(1,128)S(1)}, f32[150,1,1]{0,2,1:T(1,128)}, u32[]{:S(2)}) copy-start(f32[150,1,1]{0,2,1:T(1,128)} %get-tuple-element.233) | copy-start | bytes 1804
  57.2 5.5 %copy-start.18 = (f32[150,1,1]{0,2,1:T(1,128)S(1)}, f32[150,1,1]{0,2,1:T(1,128)}, u32[]{:S(2)}) copy-start(f32[150,1,1]{0,2,1:T(1,128)} %get-tuple-element.234) | copy-start | bytes 1804
  57.2 5.5 %copy-start.19 = (f32[150,1,1]{0,2,1:T(1,128)S(1)}, f32[150,1,1]{0,2,1:T(1,128)}, u32[]{:S(2)}) copy-start(f32[150,1,1]{0,2,1:T(1,128)} %get-tuple-element.235) | copy-start | bytes 1804
  57.2 5.5 %copy-start.20 = (f32[150,1,1]{0,2,1:T(1,128)S(1)}, f32[150,1,1]{0,2,1:T(1,128)}, u32[]{:S(2)}) copy-start(f32[150,1,1]{0,2,1:T(1,128)} %get-tuple-element.236) | copy-start | bytes 1804
  57.2 5.5 %copy-start.21 = (f32[150,1,1]{0,2,1:T(1,128)S(1)}, f32[150,1,1]{0,2,1:T(1,128)}, u32[]{:S(2)}) copy-start(f32[150,1,1]{0,2,1:T(1,128)} %get-tuple-element.237) | copy-start | bytes 1804
  57.2 5.5 %copy-start.22 = (f32[150,1,1]{0,2,1:T(1,128)S(1)}, f32[150,1,1]{0,2,1:T(1,128)}, u32[]{:S(2)}) copy-start(f32[150,1,1]{0,2,1:T(1,128)} %get-tuple-element.238) | copy-start | bytes 1804
  57.2 5.5 %copy-start.23 = (f32[150,1,1]{0,2,1:T(1,128)S(1)}, f32[150,1,1]{0,2,1:T(1,128)}, u32[]{:S(2)}) copy-start(f32[150,1,1]{0,2,1:T(1,128)} %get-tuple-element.239) | copy-start | bytes 1804
  57.2 5.5 %copy-start.24 = (f32[150,1,1]{0,2,1:T(1,128)S(1)}, f32[150,1,1]{0,2,1:T(1,128)}, u32[]{:S(2)}) copy-start(f32[150,1,1]{0,2,1:T(1,128)} %get-tuple-element.240) | copy-start | bytes 1804
  57.2 5.5 %copy-start.25 = (f32[150,1,1]{0,2,1:T(1,128)S(1)}, f32[150,1,1]{0,2,1:T(1,128)}, u32[]{:S(2)}) copy-start(f32[150,1,1]{0,2,1:T(1,128)} %get-tuple-element.241) | copy-start | bytes 1804
  57.2 5.5 %copy-start.26 = (f32[150,1,1]{0,2,1:T(1,128)S(1)}, f32[150,1,1]{0,2,1:T(1,128)}, u32[]{:S(2)}) copy-start(f32[150,1,1]{0,2,1:T(1,128)} %get-tuple-element.242) | copy-start | bytes 1804
  57.3 5.5 %copy-start.27 = (f32[150,1,1]{0,2,1:T(1,128)S(1)}, f32[150,1,1]{0,2,1:T(1,128)}, u32[]{:S(2)}) copy-start(f32[150,1,1]{0,2,1:T(1,128)} %get-tuple-element.243) | copy-start | bytes 1804
  57.3 5.5 %copy-start.28 = (f32[150,1,1]{0,2,1:T(1,128)S(1)}, f32[150,1,1]{0,2,1:T(1,128)}, u32[]{:S(2)}) copy-start(f32[150,1,1]{0,2,1:T(1,128)} %get-tuple-element.244) | copy-start | bytes 1804
  57.3 5.5 %copy-start.29 = (f32[150,1,1]{0,2,1:T(1,128)S(1)}, f32[150,1,1]{0,2,1:T(1,128)}, u32[]{:S(2)}) copy-start(f32[150,1,1]{0,2,1:T(1,128)} %get-tuple-element.245) | copy-start | bytes 1804
  57.3 5.5 %copy-start.30 = (f32[150,1,1]{0,2,1:T(1,128)S(1)}, f32[150,1,1]{0,2,1:T(1,128)}, u32[]{:S(2)}) copy-start(f32[150,1,1]{0,2,1:T(1,128)} %get-tuple-element.246) | copy-start | bytes 1804
  57.3 5.5 %copy-start.31 = (f32[150,1,1]{0,2,1:T(1,128)S(1)}, f32[150,1,1]{0,2,1:T(1,128)}, u32[]{:S(2)}) copy-start(f32[150,1,1]{0,2,1:T(1,128)} %get-tuple-element.247) | copy-start | bytes 1804
  57.3 5.5 %copy-start.32 = (f32[150,1,1]{0,2,1:T(1,128)S(1)}, f32[150,1,1]{0,2,1:T(1,128)}, u32[]{:S(2)}) copy-start(f32[150,1,1]{0,2,1:T(1,128)} %get-tuple-element.248) | copy-start | bytes 1804
  57.3 5.5 %copy-start.33 = (f32[150,1,1]{0,2,1:T(1,128)S(1)}, f32[150,1,1]{0,2,1:T(1,128)}, u32[]{:S(2)}) copy-start(f32[150,1,1]{0,2,1:T(1,128)} %get-tuple-element.249) | copy-start | bytes 1804
  57.3 5.5 %copy-start.34 = (f32[150,1,1]{0,2,1:T(1,128)S(1)}, f32[150,1,1]{0,2,1:T(1,128)}, u32[]{:S(2)}) copy-start(f32[150,1,1]{0,2,1:T(1,128)} %get-tuple-element.201) | copy-start | bytes 1804
  57.3 5.5 %copy-start.35 = (f32[150,1,1]{0,2,1:T(1,128)S(1)}, f32[150,1,1]{0,2,1:T(1,128)}, u32[]{:S(2)}) copy-start(f32[150,1,1]{0,2,1:T(1,128)} %get-tuple-element.202) | copy-start | bytes 1804
  57.3 5.5 %copy-start.36 = (f32[150,1,1]{0,2,1:T(1,128)S(1)}, f32[150,1,1]{0,2,1:T(1,128)}, u32[]{:S(2)}) copy-start(f32[150,1,1]{0,2,1:T(1,128)} %get-tuple-element.203) | copy-start | bytes 1804
  57.4 5.5 %copy-start.37 = (f32[150,1,1]{0,2,1:T(1,128)S(1)}, f32[150,1,1]{0,2,1:T(1,128)}, u32[]{:S(2)}) copy-start(f32[150,1,1]{0,2,1:T(1,128)} %get-tuple-element.204) | copy-start | bytes 1804
  57.4 5.5 %copy-start.38 = (f32[150,1,1]{0,2,1:T(1,128)S(1)}, f32[150,1,1]{0,2,1:T(1,128)}, u32[]{:S(2)}) copy-start(f32[150,1,1]{0,2,1:T(1,128)} %get-tuple-element.205) | copy-start | bytes 1804
  57.4 5.5 %copy-start.39 = (f32[150,1,1]{0,2,1:T(1,128)S(1)}, f32[150,1,1]{0,2,1:T(1,128)}, u32[]{:S(2)}) copy-start(f32[150,1,1]{0,2,1:T(1,128)} %get-tuple-element.206) | copy-start | bytes 1804
  57.4 5.5 %copy-start.40 = (f32[150,1,1]{0,2,1:T(1,128)S(1)}, f32[150,1,1]{0,2,1:T(1,128)}, u32[]{:S(2)}) copy-start(f32[150,1,1]{0,2,1:T(1,128)} %get-tuple-element.207) | copy-start | bytes 1804
  104.2 6.3 %copy-start.47 = (bf16[150,600]{1,0:T(8,128)(2,1)S(1)}, bf16[150,600]{1,0:T(8,128)(2,1)}, u32[]{:S(2)}) copy-start(bf16[150,600]{1,0:T(8,128)(2,1)} %param.16) | copy-start | bytes 540004
  104.2 6.3 %copy-start.48 = (f32[150]{0:T(256)S(1)}, f32[150]{0:T(256)}, u32[]{:S(2)}) copy-start(f32[150]{0:T(256)} %param.15) | copy-start | bytes 1804
  126.8 6.6 %copy-start.5 = (f32[2,150,512]{2,0,1:T(2,128)S(1)}, f32[2,150,512]{2,0,1:T(2,128)}, u32[]{:S(2)}) copy-start(f32[2,150,512]{2,0,1:T(2,128)} %param.18) | copy-start | bytes 1843204
  129.6 20.0 %all-to-all-start = ((bf16[150,16,256]{2,0,1:T(8,128)(2,1)}), bf16[150,16,256]{2,0,1:T(8,128)(2,1)S(1)}, u32[]{:S(2)}, u32[]{:S(2)}) async-start(bf16[150,16,256]{2,0,1:T(8,128)(2,1)} %copy.43), calls=%async_computation | async-start | bytes 2490368 | tf_op jit(solution)/shard_map/all_to_all | solution.py:110
  157.5 7.0 %copy-start.2 = (bf16[150,16,256]{2,1,0:T(8,128)(2,1)S(1)}, bf16[150,16,256]{2,1,0:T(8,128)(2,1)}, u32[]{:S(2)}) copy-start(bf16[150,16,256]{2,1,0:T(8,128)(2,1)} %get-tuple-element.144) | copy-start | bytes 3686404
  160.0 30.2 %all-to-all-start.1 = ((bf16[150,4,1024]{0,1,2:T(4,128)(2,1)}), bf16[150,4,1024]{0,1,2:T(4,128)(2,1)}, u32[]{:S(2)}, u32[]{:S(2)}) async-start(bf16[150,4,1024]{0,1,2:T(4,128)(2,1)} %copy.46), calls=%async_computation.1 | async-start | bytes 4194304 | tf_op jit(solution)/shard_map/all_to_all | solution.py:124
  (7 other events, 30.3 us)
where the time goes:
time: 206 us; the launch traced here: 203 us
  other arithmetic  68.6 us (33%)
  local copies, waits for them, and re-layouts  60 us (29%)
  waiting for transfers between devices  33.6 us (16%)
  starting transfers between devices  17.2 us (8%)
  matrix products  12.6 us (6%)
  blocking collectives  10.2 us (5%)
    add x1, other arithmetic, depthwise_conv(): total + weight_col * extended[:, tap_row:tap_row + lat_rows, tap_col:tap_...  41.2 us
    all_to_all x1, waiting for transfers between devices, local(): lax.all_to_all(along_rows, 'lon', split_axis=2, concat_axis=1, tiled=True)  23.3 us
    while x3, local copies, waits for them, and re-layouts, local(): lax.fori_loop(0, lat_rows // group_rows, mix_rows, jnp.zeros(field.shape,...  11.2 us
    all_gather x1, blocking collectives, local(): fold_full = lax.all_gather(top_rows, 'lon', axis=2, tiled=True)  10.2 us
    another operation x2, other arithmetic  9.82 us
    unnamed x103, local copies, waits for them, and re-layouts  8.46 us
    all_to_all x1, waiting for transfers between devices, local(): lax.all_to_all(residual, 'lon', split_axis=1, concat_axis=2, tiled=True)  6.4 us
    all_to_all x1, local copies, waits for them, and re-layouts, local(): lax.all_to_all(along_rows, 'lon', split_axis=2, concat_axis=1, tiled=True)  6.32 us
  transfers between devices with their start and end apart: 6, of which 3 were waited for; matrix products, arithmetic and copies ran while one was open for 17% of the time, Pallas kernels for 0%

commit v1 on v0

v1 whole, which is shorter than its diff:
```python
import functools
import math

import jax
import jax.numpy as jnp
import numpy as np
from jax import lax
from jax.experimental import pallas as pl
from jax.experimental.pallas import tpu as pltpu
from jax.sharding import PartitionSpec as P

F32 = jnp.float32
BF16 = jnp.bfloat16
TAPS = 7
HALO = 3
LANES = 128


def dft_table(lon_points, mode_count):
    phase = np.arange(lon_points)[:, None] * np.arange(mode_count)[None, :] % lon_points
    angles = phase.astype(np.float32) * np.float32(2.0 * math.pi / lon_points)
    factor = np.float32(1.0 / math.sqrt(lon_points))
    angles = angles.astype(np.float64)
    table = np.concatenate([np.cos(angles), -np.sin(angles)], axis=1).astype(np.float32)
    return (table * factor).astype(BF16)


def kernel(
    sizes,
    field_ref, mask_ref, fold_ref, taps_ref, gain_ref, w_in_ref, w_out_ref, mix_ref, spec_hbm, table_hbm,
    out_ref,
    flat, ext, own, depth, res, by_rows, back, spatial,
    edge_mine, edge_left, edge_right, comb, comb_n, comb_s, rows_n, rows_s, top_all,
    spec_ref, table_ref,
    local_sem, edge_send, edge_recv, comb_send, comb_recv, rows_send, rows_recv,
    fold_send, fold_recv, out_send, out_recv, in_send, in_recv,
):
    channels, padded, rows, cols, lat_n, lon_n, modes = sizes
    lon_points = cols * lon_n
    per = rows // lon_n
    lat = lax.axis_index("lat")
    lon = lax.axis_index("lon")
    left = lax.rem(lon + lon_n - 1, lon_n)
    right = lax.rem(lon + 1, lon_n)
    chip = lon // 2
    core = lax.rem(lon, 2)
    chips = lon_n // 2

    def target(k):
        return lax.rem(chip + k // 2, chips) * 2 + lax.rem(core + lax.rem(k, 2), 2)

    def source(k):
        return lax.rem(chip + chips - k // 2, chips) * 2 + lax.rem(core + lax.rem(k, 2), 2)

    table_copy = pltpu.make_async_copy(table_hbm, table_ref, local_sem.at[0])
    spec_copy = pltpu.make_async_copy(spec_hbm, spec_ref, local_sem.at[1])
    table_copy.start()
    spec_copy.start()

    barrier = pltpu.get_barrier_semaphore()
    for k in range(1, lon_n):
        pl.semaphore_signal(barrier, inc=1, device_id={"lon": target(k)})

    @pl.when(lat > 0)
    def _():
        pl.semaphore_signal(barrier, inc=1, device_id={"lat": lat - 1})

    @pl.when(lat < lat_n - 1)
    def _():
        pl.semaphore_signal(barrier, inc=1, device_id={"lat": lat + 1})

    wet = mask_ref[...].astype(F32)

    @pl.loop(0, channels)
    def _(c):
        val = field_ref[c].astype(F32) * wet
        at = pl.multiple_of(c * rows, rows)
        flat[0, pl.ds(at, rows), :] = val[:, :LANES]
        flat[1, pl.ds(at, rows), :] = val[:, LANES:]

    tail = (padded - channels) * rows
    if tail:
        for h in range(2):
            flat[h, channels * rows :, :] = jnp.zeros((tail, LANES), F32)

    lane = lax.broadcasted_iota(jnp.int32, (padded, LANES), 1)
    pack = jnp.zeros((padded, LANES), F32)
    edge_mine[...] = pack.astype(BF16)
    for i in range(rows):
        lo = flat[0, pl.ds(i, padded, stride=rows), :]
        hi = flat[1, pl.ds(i, padded, stride=rows), :]
        own[i, :, :LANES] = lo.astype(BF16)
        own[i, :, LANES:] = hi.astype(BF16)
        ext[i + HALO, :, :LANES] = lo
        ext[i + HALO, :, LANES : 2 * LANES] = hi
        edge = jnp.where(lane < HALO, lo, jnp.where(lane >= LANES - HALO, hi, 0.0))
        if i:
            edge = pltpu.roll(edge, 8 * i, 1)
        edge_mine[...] = (edge_mine[...].astype(F32) + edge).astype(BF16)

    count = lon_n - 1 + jnp.where(lat > 0, 1, 0) + jnp.where(lat < lat_n - 1, 1, 0)
    pl.semaphore_wait(barrier, count)

    to_left = pltpu.make_async_remote_copy(
        edge_mine, edge_right, edge_send.at[0], edge_recv.at[0], device_id={"lon": left})
    to_right = pltpu.make_async_remote_copy(
        edge_mine, edge_left, edge_send.at[1], edge_recv.at[1], device_id={"lon": right})
    to_left.start()
    to_right.start()

    rows_down = pltpu.make_async_remote_copy(
        own.at[pl.ds(0, HALO)], rows_n, rows_send.at[0], rows_recv.at[0], device_id={"lat": lat - 1})
    rows_up = pltpu.make_async_remote_copy(
        own.at[pl.ds(rows - HALO, HALO)], rows_s, rows_send.at[1], rows_recv.at[1], device_id={"lat": lat + 1})
    comb_down = pltpu.make_async_remote_copy(
        comb, comb_n, comb_send.at[0], comb_recv.at[0], device_id={"lat": lat - 1})
    comb_up = pltpu.make_async_remote_copy(
        comb, comb_s, comb_send.at[1], comb_recv.at[1], device_id={"lat": lat + 1})

    def fold_copy(k):
        at = pl.multiple_of(lon * cols, LANES)
        return pltpu.make_async_remote_copy(
            own.at[pl.ds(rows - HALO, HALO)], top_all.at[:, :, pl.ds(at, cols)],
            fold_send.at[k - 1], fold_recv.at[k - 1], device_id={"lon": target(k)})

    @pl.when(lat > 0)
    def _():
        rows_down.start()

    @pl.when(lat < lat_n - 1)
    def _():
        rows_up.start()

    @pl.when(lat == lat_n - 1)
    def _():
        for k in range(lon_n - 1, 0, -1):
            fold_copy(k).start()
        top_all[:, :, pl.ds(pl.multiple_of(lon * cols, LANES), cols)] = own[rows - HALO :]

    to_left.wait()
    to_right.wait()
    both = jnp.where(lax.rem(lane, 8) < 4, edge_right[...].astype(F32), edge_left[...].astype(F32))
    comb[...] = both.astype(BF16)

    @pl.when(lat > 0)
    def _():
        comb_down.start()

    @pl.when(lat < lat_n - 1)
    def _():
        comb_up.start()

    def edges_of(packed, i):
        return pltpu.roll(packed, LANES - 8 * i, 1) if i else packed

    for i in range(rows):
        ext[i + HALO, :, 2 * LANES :] = edges_of(comb[...].astype(F32), i)

    def conv(out_rows):
        lo_e, hi_e = min(out_rows), max(out_rows) + TAPS

        @pl.loop(0, padded // 8)
        def _(group):
            at = pl.multiple_of(group * 8, 8)
            taps = taps_ref[pl.ds(at, 8), :]
            acc = {}
            for b in range(TAPS):
                weights = [
                    jnp.broadcast_to(taps[:, a * TAPS + b : a * TAPS + b + 1], (8, cols))
                    for a in range(TAPS)
                ]
                for e in range(lo_e, hi_e):
                    line = ext[e, pl.ds(at, 8), :]
                    if b != HALO:
                        line = pltpu.roll(line, (HALO - b) % (cols + LANES), 1)
                    line = line[:, :cols]
                    for a in range(TAPS):
                        i = e - a
                        if i in out_rows:
                            term = weights[a] * line
                            acc[i] = acc[i] + term if i in acc else term
            for i in out_rows:
                depth[i, pl.ds(at, 8), :] = acc[i]

    conv(list(range(HALO, rows - HALO)))

    @pl.when(lat > 0)
    def _():
        rows_down.wait_send()
        comb_down.wait_send()
        rows_up.wait_recv()
        comb_up.wait_recv()
        for r in range(HALO):
            ext[r, :, :cols] = rows_s[r].astype(F32)
            ext[r, :, cols:] = edges_of(comb_s[...].astype(F32), rows - HALO + r)

    @pl.when(lat == 0)
    def _():
        for r in range(HALO):
            ext[r] = jnp.zeros((padded, cols + LANES), F32)

    @pl.when(lat < lat_n - 1)
    def _():
        rows_up.wait_send()
        comb_up.wait_send()
        rows_down.wait_recv()
        comb_down.wait_recv()
        for r in range(HALO):
            ext[rows + HALO + r, :, :cols] = rows_n[r].astype(F32)
            ext[rows + HALO + r, :, cols:] = edges_of(comb_n[...].astype(F32), r)

    @pl.when(lat == lat_n - 1)
    def _():
        for k in range(lon_n - 1, 0, -1):
            fold_copy(k).wait()
        point = lax.broadcasted_iota(jnp.int32, (lon_points, cols + LANES), 0)
        pick = jnp.where(point == fold_ref[...], 1.0, 0.0).astype(BF16)
        for r in range(HALO):
            ext[rows + HALO + r] = jnp.dot(top_all[HALO - 1 - r], pick, preferred_element_type=F32)

    conv(list(range(HALO)))
    conv(list(range(rows - HALO, rows)))

    inside = lax.broadcasted_iota(jnp.int32, (padded, cols), 0) < channels

    def send_row(t):
        k = lon_n - 1 - t // per
        row = target(k) * per + lax.rem(t, per)
        return pltpu.make_async_remote_copy(
            res.at[row], by_rows.at[lax.rem(t, per), :, pl.ds(pl.multiple_of(lon * cols, LANES), cols)],
            out_send.at[t], out_recv.at[t], device_id={"lon": target(k)})

    @pl.loop(0, rows)
    def _(t):
        k = lon_n - 1 - t // per
        row = target(k) * per + lax.rem(t, per)
        x = depth[row]
        mean = jnp.sum(x, axis=0, keepdims=True) * (1.0 / channels)
        centred = jnp.where(inside, x - mean, 0.0)
        var = jnp.sum(centred * centred, axis=0, keepdims=True) * (1.0 / channels)
        normed = (centred * lax.rsqrt(var + 1e-06) * gain_ref[...]).astype(BF16)
        pre = jnp.dot(w_in_ref[...], normed, preferred_element_type=F32)
        hidden = jax.nn.gelu(pre, approximate=True).astype(BF16)
        branch = jnp.dot(w_out_ref[...], hidden, preferred_element_type=F32)
        wet_row = mask_ref[pl.ds(row, 1), :].astype(F32)
        val = (wet_row * (own[row].astype(F32) + branch)).astype(BF16)
        res[row] = val

        @pl.when(t < (lon_n - 1) * per)
        def _():
            send_row(t).start()

        @pl.when(t >= (lon_n - 1) * per)
        def _():
            by_rows[lax.rem(t, per), :, pl.ds(pl.multiple_of(lon * cols, LANES), cols)] = val

    table_copy.wait()
    spec_copy.wait()

    def send_back(r, k):
        q = target(k)
        s = (lon_n - 1 - k) * per + r
        return pltpu.make_async_remote_copy(
            back.at[r, :, pl.ds(pl.multiple_of(q * cols, LANES), cols)], spatial.at[lon * per + r],
            in_send.at[s], in_recv.at[s], device_id={"lon": q})

    @pl.loop(0, per)
    def _(r):
        for kk in range(lon_n - 1):
            send_row(kk * per + r).wait_recv()
        spectrum = jnp.dot(by_rows[r], table_ref[...], preferred_element_type=F32)
        s_re = spectrum[:, :modes]
        s_im = spectrum[:, modes:]
        g_re = spec_ref[0]
        g_im = spec_ref[1]
        scaled = jnp.concatenate(
            [(g_re * s_re - g_im * s_im).astype(BF16), (g_re * s_im + g_im * s_re).astype(BF16)], axis=1)
        back[r] = lax.dot_general(
            scaled, table_ref[...], (((1,), (1,)), ((), ())), preferred_element_type=F32).astype(BF16)
        for k in range(lon_n - 1, 0, -1):
            send_back(r, k).start()
        spatial[lon * per + r] = back[r, :, pl.ds(pl.multiple_of(lon * cols, LANES), cols)]

    @pl.loop(0, rows)
    def _(t):
        k = t // per
        row = source(k) * per + lax.rem(t, per)

        @pl.when(t >= per)
        def _():
            send_back(lax.rem(t, per), k).wait_recv()

        mixed = jnp.dot(mix_ref[...], spatial[row], preferred_element_type=F32)
        wet_row = mask_ref[pl.ds(row, 1), :].astype(F32)
        val = wet_row * (res[row].astype(F32) + mixed)
        flat[0, pl.ds(row, padded, stride=rows), :] = val[:, :LANES]
        flat[1, pl.ds(row, padded, stride=rows), :] = val[:, LANES:]

    @pl.loop(0, channels)
    def _(c):
        at = pl.multiple_of(c * rows, rows)
        out_ref[c, :, :LANES] = flat[0, pl.ds(at, rows), :].astype(BF16)
        out_ref[c, :, LANES:] = flat[1, pl.ds(at, rows), :].astype(BF16)

    @pl.loop(0, (lon_n - 1) * per)
    def _(t):
        send_row(t).wait_send()
        send_back(lax.rem(t, per), lon_n - 1 - t // per).wait_send()


def local(lat_n, lon_n, field, land_mask, fold_partner, dw_kernel, norm_gain, w_in, w_out, spec_gain, mix_weight):
    channels, rows, cols = field.shape
    modes = spec_gain.shape[2]
    hid = w_in.shape[1]
    lon_points = cols * lon_n
    padded = -(-channels // 16) * 16
    hid_pad = -(-hid // 16) * 16
    extra = padded - channels
    table = jnp.asarray(dft_table(lon_points, modes))
    lane = jnp.arange(cols + LANES, dtype=jnp.int32)
    column = jnp.where(lane < cols + HALO, lane, lane - (cols + LANES))
    fold = (fold_partner[0] - (lax.axis_index("lon") * cols + column)) % lon_points
    taps = jnp.pad(dw_kernel.reshape(channels, -1), ((0, extra), (0, LANES - TAPS * TAPS)))
    gain = jnp.pad(norm_gain, (0, extra))[:, None]
    w_in_t = jnp.pad(w_in.T, ((0, hid_pad - hid), (0, extra)))
    w_out_t = jnp.pad(w_out.T, ((0, extra), (0, hid_pad - hid)))
    mix_t = jnp.pad(mix_weight.T, ((0, extra), (0, extra)))
    spec = jnp.pad(spec_gain, ((0, 0), (0, extra), (0, 0)))
    per = rows // lon_n
    sizes = (channels, padded, rows, cols, lat_n, lon_n, modes)
    vmem = pl.BlockSpec(memory_space=pltpu.VMEM)
    hbm = pl.BlockSpec(memory_space=pl.ANY)
    dma = pltpu.SemaphoreType.DMA
    peers = lon_n - 1
    return pl.pallas_call(
        functools.partial(kernel, sizes),
        out_shape=jax.ShapeDtypeStruct(field.shape, BF16),
        in_specs=[vmem] * 8 + [hbm] * 2,
        out_specs=vmem,
        scratch_shapes=[
            pltpu.VMEM((2, padded * rows, LANES), F32),
            pltpu.VMEM((rows + 2 * HALO, padded, cols + LANES), F32),
            pltpu.VMEM((rows, padded, cols), BF16),
            pltpu.VMEM((rows, padded, cols), F32),
            pltpu.VMEM((rows, padded, cols), BF16),
            pltpu.VMEM((per, padded, lon_points), BF16),
            pltpu.VMEM((per, padded, lon_points), BF16),
            pltpu.VMEM((rows, padded, cols), BF16),
            *[pltpu.VMEM((padded, LANES), BF16)] * 6,
            *[pltpu.VMEM((HALO, padded, cols), BF16)] * 2,
            pltpu.VMEM((HALO, padded, lon_points), BF16),
            pltpu.VMEM(spec.shape, F32),
            pltpu.VMEM(table.shape, BF16),
            *[dma((2,))] * 7,
            *[dma((peers,))] * 2,
            *[dma((peers * per,))] * 4,
        ],
        compiler_params=pltpu.CompilerParams(
            collective_id=0, has_side_effects=True, vmem_limit_bytes=62 * 1024 * 1024),
        name="block",
    )(field, land_mask, fold[None, :], taps, gain, w_in_t, w_out_t, mix_t, spec, table)


def solution(mesh):
    placed = (P(None, "lat", "lon"), P("lat", "lon"), P(), P(), P(), P(), P(), P(), P())
    return jax.shard_map(
        functools.partial(local, mesh.shape["lat"], mesh.shape["lon"]),
        mesh=mesh, in_specs=placed, out_specs=P(None, "lat", "lon"), check_vma=False,
    )
```

time: 206 us -> 80.5 us (0.39)
  other arithmetic: 68.6 us -> 1.24 us
  Pallas kernels: 0 us -> 65.8 us
  local copies, waits for them, and re-layouts: 60 us -> 11.9 us
  waiting for transfers between devices: 33.6 us -> 0 us
  starting transfers between devices: 17.2 us -> 0 us
  matrix products: 12.6 us -> 0 us
  blocking collectives: 10.2 us -> 0 us
    pallas_call x0 -> x1, Pallas kernels: none -> 65.8 us  [local(): pl.pallas_call(functools.partial(kernel, sizes), out_shape=jax.ShapeDtype...]
    add x1 -> x0, other arithmetic: 41.2 us -> none  [depthwise_conv(): total + weight_col * extended[:, tap_row:tap_row + lat_rows, tap_col:tap_...]
    all_to_all x2 -> x0, waiting for transfers between devices: 29.7 us -> none  [the longest x1 23.3 us: local(): lax.all_to_all(along_rows, 'lon', split_axis=2, concat_axis=1, tiled=True)]
    while x19 -> x0, local copies, waits for them, and re-layouts: 13.6 us -> none  [the longest x3 11.2 us: local(): lax.fori_loop(0, lat_rows // group_rows, mix_rows, jnp.zeros(field.shape,...]
    dot_general x5 -> x0, matrix products: 12.6 us -> none  [the longest x2 6.27 us: point_mixer(): jnp.einsum('hc,hp->cp', w_out, hidden, preferred_element_type=jnp.float32)]
    all_gather x1 -> x0, blocking collectives: 10.2 us -> none  [local(): fold_full = lax.all_gather(top_rows, 'lon', axis=2, tiled=True)]
    another operation x2 -> x0, other arithmetic: 9.82 us -> none
    ppermute x4 -> x0, starting transfers between devices: 8.99 us -> none  [the longest x2 5.78 us: extended_2(): lax.ppermute(tail, axis, [(i, (i + 1) % count) for i in range(ends)])]
  transfers between devices with their start and end apart: 6 -> 0, of which waited for: 3 -> 0; matrix products, arithmetic and copies ran while one was open for 17% -> 0% of each run, Pallas kernels for 0% -> 0%
where the time goes in v1:
time: 80.5 us; the launch traced here: 79 us
  Pallas kernels  65.8 us (82%)
  local copies, waits for them, and re-layouts  11.9 us (15%)
  other arithmetic  1.24 us (2%)
    pallas_call x1, Pallas kernels, local(): pl.pallas_call(functools.partial(kernel, sizes), out_shape=jax.ShapeDtype...  65.8 us
    unnamed x8, local copies, waits for them, and re-layouts  3.68 us
    pad x1, local copies, waits for them, and re-layouts, local(): w_out_t = jnp.pad(w_out.T, ((0, extra), (0, hid_pad - hid)))  1.63 us

profile of v1, /device:TPU:0, one launch (start us, length us, event | category | flops | bytes accessed | tf_op | source)
XLA Modules:
  0.0 79.0 jit_solution(12300304032985781284)
XLA Ops:
  0.0 0.0 copy-start
  0.0 0.0 copy-start.1
  0.0 1.3 %slice.3 = s32[1]{0:T(128)} slice(s32[1024]{0:T(1024)} %param.12), slice={[0:1]} | slice | bytes 8 | tf_op jit(solution)/shard_map/slice | solution.py:322
  1.3 1.2 %and_select_fusion.fold_ref = s32[1,384]{1,0:T(1,128)} fusion(s32[]{:T(128)S(6)} %mul.3, s32[]{:T(128)} %bitcast), kind=kLoop, calls=%fused_computation.3 | loop fusion | flops 6144 | bytes 1544 | tf_op jit(solution)/shard_map/jit(remainder)/select_n | solution.py:322
  2.5 0.7 pad.25
  3.2 0.8 %reshape.61 = f32[150,49]{0,1:T(8,128)S(1)} reshape(f32[150,7,7]{0,2,1:T(8,128)} %param.13) | data formatting | bytes 58800 | tf_op jit(solution)/shard_map/reshape | solution.py:323
  4.0 0.1 copy.15
  4.1 0.6 pad.24.taps_ref
  4.8 1.0 %copy.17 = bf16[150,150]{0,1:T(8,128)(2,1)S(1)} copy(bf16[150,150]{1,0:T(8,128)(2,1)} %param.18) | data formatting | bytes 90000 | tf_op args[8]
  5.8 0.6 pad.28.mix_ref
  6.4 0.7 copy.19.gain_ref
  7.2 1.6 %pad.27.w_out_ref = bf16[160,608]{1,0:T(8,128)(2,1)} pad(bf16[150,600]{1,0:T(8,128)(2,1)} %bitcast.9, bf16[]{:T(256)} %constant.32.clone.1), padding=0_10x0_8 | pad | bytes 374562 | tf_op jit(solution)/shard_map/jit(_pad)/pad | solution.py:326
  8.8 0.0 copy-done.1
  8.8 0.2 copy.16
  9.0 0.8 pad.26.w_in_ref
  9.7 0.0 copy-done
  9.7 0.1 copy.18
  9.9 0.9 %pad.29.spec_hbm = f32[2,160,512]{2,1,0:T(8,128)} pad(f32[2,150,512]{2,1,0:T(8,128)S(1)} %copy.18, f32[]{:T(128)} %constant.31.clone.1), padding=0_0x0_10x0_0 | pad | bytes 1269764 | tf_op jit(solution)/shard_map/jit(_pad)/pad | solution.py:328
  10.8 65.8 %block.1 = bf16[150,16,256]{2,1,0:T(8,128)(2,1)} custom-call(bf16[150,16,256]{2,1,0:T(8,128)(2,1)} %field_ref.1, s32[16,256]{1,0:T(8,128)} %mask_ref.1, s32[1,384]{1,0:T(1,128)} %and_select_fusion.fold_ref, f32[160,128]{1,0:T(8,128)} %pad.24.taps_ref, f32[160,1]{1,0:T(8,128)} %copy.19.gain_ref, bf16[608,160]{1,0:T(8,128)(2,1)} %pad.26.w_in_ref, ...), custom_call_target="tpu_custom_call" | custom-call | tf_op jit(solution)/shard_map/block/pallas_call | solution.py:335
  76.6 2.4 %copy.21 = bf16[150,16,256]{2,1,0:T(8,128)(2,1)} copy(bf16[150,16,256]{2,1,0:T(8,128)(2,1)} %block.1) | data formatting | bytes 2457600
Async XLA Ops:
  0.0 9.7 %copy-start = (f32[2,150,512]{2,0,1:T(2,128)S(1)}, f32[2,150,512]{2,0,1:T(2,128)}, u32[]{:S(2)}) copy-start(f32[2,150,512]{2,0,1:T(2,128)} %param.17) | copy-start | bytes 1843204
  0.0 8.8 %copy-start.1 = (bf16[150,600]{1,0:T(8,128)(2,1)S(1)}, bf16[150,600]{1,0:T(8,128)(2,1)}, u32[]{:S(2)}) copy-start(bf16[150,600]{1,0:T(8,128)(2,1)} %param.15) | copy-start | bytes 540004

commit v2 on v1

v2 whole, which is shorter than its diff:
```python
import functools
import math

import jax
import jax.numpy as jnp
import numpy as np
from jax import lax
from jax.experimental import pallas as pl
from jax.experimental.pallas import tpu as pltpu
from jax.sharding import PartitionSpec as P

F32 = jnp.float32
BF16 = jnp.bfloat16
TAPS = 7
HALO = 3
LANES = 128


def dft_table(lon_points, mode_count):
    phase = np.arange(lon_points)[:, None] * np.arange(mode_count)[None, :] % lon_points
    angles = phase.astype(np.float32) * np.float32(2.0 * math.pi / lon_points)
    factor = np.float32(1.0 / math.sqrt(lon_points))
    angles = angles.astype(np.float64)
    table = np.concatenate([np.cos(angles), -np.sin(angles)], axis=1).astype(np.float32)
    return (table * factor).astype(BF16)


def kernel(
    sizes,
    field_ref, mask_ref, fold_ref, taps_ref, gain_ref, w_in_ref, w_out_ref, mix_ref, spec_hbm, table_hbm,
    out_ref,
    flat, ext, own, depth, res, by_rows, back, spatial,
    edge_mine, edge_left, edge_right, comb, comb_n, comb_s, rows_n, rows_s, top_all,
    spec_ref, table_ref, wide_taps, w_in_t, w_out_t, mix_t, gain_col,
    local_sem, edge_send, edge_recv, comb_send, comb_recv, rows_send, rows_recv,
    fold_send, fold_recv, out_send, out_recv, in_send, in_recv,
):
    channels, padded, rows, cols, lat_n, lon_n, modes = sizes
    lon_points = cols * lon_n
    per = rows // lon_n
    lat = lax.axis_index("lat")
    lon = lax.axis_index("lon")
    left = lax.rem(lon + lon_n - 1, lon_n)
    right = lax.rem(lon + 1, lon_n)
    chip = lon // 2
    core = lax.rem(lon, 2)
    chips = lon_n // 2

    def target(k):
        return lax.rem(chip + k // 2, chips) * 2 + lax.rem(core + lax.rem(k, 2), 2)

    def source(k):
        return lax.rem(chip + chips - k // 2, chips) * 2 + lax.rem(core + lax.rem(k, 2), 2)

    table_copy = pltpu.make_async_copy(table_hbm, table_ref, local_sem.at[0])
    spec_copy = pltpu.make_async_copy(spec_hbm, spec_ref, local_sem.at[1])
    table_copy.start()
    spec_copy.start()

    barrier = pltpu.get_barrier_semaphore()
    for k in range(1, lon_n):
        pl.semaphore_signal(barrier, inc=1, device_id={"lon": target(k)})

    @pl.when(lat > 0)
    def _():
        pl.semaphore_signal(barrier, inc=1, device_id={"lat": lat - 1})

    @pl.when(lat < lat_n - 1)
    def _():
        pl.semaphore_signal(barrier, inc=1, device_id={"lat": lat + 1})

    wet = mask_ref[...].astype(F32)

    @pl.loop(0, channels)
    def _(c):
        val = field_ref[c].astype(F32) * wet
        at = pl.multiple_of(c * rows, rows)
        flat[0, pl.ds(at, rows), :] = val[:, :LANES]
        flat[1, pl.ds(at, rows), :] = val[:, LANES:]

    tail = (padded - channels) * rows
    if tail:
        for h in range(2):
            flat[h, channels * rows :, :] = jnp.zeros((tail, LANES), F32)

    lane = lax.broadcasted_iota(jnp.int32, (padded, LANES), 1)
    pack = jnp.zeros((padded, LANES), F32)
    edge_mine[...] = pack.astype(BF16)
    for i in range(rows):
        lo = flat[0, pl.ds(i, padded, stride=rows), :]
        hi = flat[1, pl.ds(i, padded, stride=rows), :]
        own[i, :, :LANES] = lo.astype(BF16)
        own[i, :, LANES:] = hi.astype(BF16)
        ext[i + HALO, :, :LANES] = lo
        ext[i + HALO, :, LANES : 2 * LANES] = hi
        edge = jnp.where(lane < HALO, lo, jnp.where(lane >= LANES - HALO, hi, 0.0))
        if i:
            edge = pltpu.roll(edge, 8 * i, 1)
        edge_mine[...] = (edge_mine[...].astype(F32) + edge).astype(BF16)

    count = lon_n - 1 + jnp.where(lat > 0, 1, 0) + jnp.where(lat < lat_n - 1, 1, 0)
    pl.semaphore_wait(barrier, count)

    to_left = pltpu.make_async_remote_copy(
        edge_mine, edge_right, edge_send.at[0], edge_recv.at[0], device_id={"lon": left})
    to_right = pltpu.make_async_remote_copy(
        edge_mine, edge_left, edge_send.at[1], edge_recv.at[1], device_id={"lon": right})
    to_left.start()
    to_right.start()

    rows_down = pltpu.make_async_remote_copy(
        own.at[pl.ds(0, HALO)], rows_n, rows_send.at[0], rows_recv.at[0], device_id={"lat": lat - 1})
    rows_up = pltpu.make_async_remote_copy(
        own.at[pl.ds(rows - HALO, HALO)], rows_s, rows_send.at[1], rows_recv.at[1], device_id={"lat": lat + 1})
    comb_down = pltpu.make_async_remote_copy(
        comb, comb_n, comb_send.at[0], comb_recv.at[0], device_id={"lat": lat - 1})
    comb_up = pltpu.make_async_remote_copy(
        comb, comb_s, comb_send.at[1], comb_recv.at[1], device_id={"lat": lat + 1})

    def fold_copy(k):
        at = pl.multiple_of(lon * cols, LANES)
        return pltpu.make_async_remote_copy(
            own.at[pl.ds(rows - HALO, HALO)], top_all.at[:, :, pl.ds(at, cols)],
            fold_send.at[k - 1], fold_recv.at[k - 1], device_id={"lon": target(k)})

    @pl.when(lat > 0)
    def _():
        rows_down.start()

    @pl.when(lat < lat_n - 1)
    def _():
        rows_up.start()

    @pl.when(lat == lat_n - 1)
    def _():
        for k in range(lon_n - 1, 0, -1):
            fold_copy(k).start()
        top_all[:, :, pl.ds(pl.multiple_of(lon * cols, LANES), cols)] = own[rows - HALO :]

    wide_taps[:, padded - 16 :, :] = jnp.zeros((TAPS * TAPS, 16, LANES), F32)
    for t in range(TAPS * TAPS):
        wide_taps[t, :channels, :] = jnp.broadcast_to(taps_ref[:, t : t + 1], (channels, LANES))

    def turned(ref, target_ref):
        n, m = ref.shape
        up = [-(-d // LANES) * LANES for d in (n, m)]
        full = jnp.concatenate([ref[...].astype(F32), jnp.zeros((n, up[1] - m), F32)], axis=1)
        full = jnp.concatenate([full, jnp.zeros((up[0] - n, up[1]), F32)], axis=0)
        target_ref[...] = full.T[: target_ref.shape[0], : target_ref.shape[1]].astype(BF16)

    turned(w_in_ref, w_in_t)
    turned(w_out_ref, w_out_t)
    turned(mix_ref, mix_t)
    diagonal = lax.broadcasted_iota(jnp.int32, (padded, channels), 0) == lax.broadcasted_iota(
        jnp.int32, (padded, channels), 1)
    gain_col[...] = jnp.broadcast_to(
        jnp.sum(jnp.where(diagonal, gain_ref[...], 0.0), axis=1, keepdims=True), (padded, LANES))
    back[:, padded - 16 :, :] = jnp.zeros((per, 16, lon_points), BF16)

    to_left.wait()
    to_right.wait()
    both = jnp.where(lax.rem(lane, 8) < 4, edge_right[...].astype(F32), edge_left[...].astype(F32))
    comb[...] = both.astype(BF16)

    @pl.when(lat > 0)
    def _():
        comb_down.start()

    @pl.when(lat < lat_n - 1)
    def _():
        comb_up.start()

    def edges_of(packed, i):
        return pltpu.roll(packed, LANES - 8 * i, 1) if i else packed

    for i in range(rows):
        ext[i + HALO, :, 2 * LANES :] = edges_of(comb[...].astype(F32), i)

    def conv(out_rows):
        lines = sorted({i + a for i in out_rows for a in range(TAPS)})

        @pl.loop(0, padded // 16)
        def _(group):
            for half in range(2):
                at = pl.multiple_of(group * 16 + half * 8, 8)
                acc = {}
                for b in range(TAPS):
                    weights = [wide_taps[a * TAPS + b, pl.ds(at, 8), :] for a in range(TAPS)]
                    for e in lines:
                        line = ext[e, pl.ds(at, 8), :]
                        if b != HALO:
                            line = pltpu.roll(line, (HALO - b) % (cols + LANES), 1)
                        for a in range(TAPS):
                            i = e - a
                            if i in out_rows:
                                for h in range(cols // LANES):
                                    term = weights[a] * line[:, h * LANES : (h + 1) * LANES]
                                    acc[i, h] = acc[i, h] + term if (i, h) in acc else term
                for (i, h), total in acc.items():
                    depth[i, pl.ds(at, 8), h * LANES : (h + 1) * LANES] = total

    def await_halo():
        @pl.when(lat > 0)
        def _():
            rows_down.wait_send()
            comb_down.wait_send()
            rows_up.wait_recv()
            comb_up.wait_recv()
            for r in range(HALO):
                ext[r, :, :cols] = rows_s[r].astype(F32)
                ext[r, :, cols:] = edges_of(comb_s[...].astype(F32), rows - HALO + r)

        @pl.when(lat == 0)
        def _():
            for r in range(HALO):
                ext[r] = jnp.zeros((padded, cols + LANES), F32)

        @pl.when(lat < lat_n - 1)
        def _():
            rows_up.wait_send()
            comb_up.wait_send()
            rows_down.wait_recv()
            comb_down.wait_recv()
            for r in range(HALO):
                ext[rows + HALO + r, :, :cols] = rows_n[r].astype(F32)
                ext[rows + HALO + r, :, cols:] = edges_of(comb_n[...].astype(F32), r)

        @pl.when(lat == lat_n - 1)
        def _():
            for k in range(lon_n - 1, 0, -1):
                fold_copy(k).wait()
            point = lax.broadcasted_iota(jnp.int32, (lon_points, cols + LANES), 0)
            at = lax.broadcasted_iota(jnp.int32, (1, cols + LANES), 1)
            at = jnp.where(at < cols + HALO, at, at - (cols + LANES)) + lon * cols
            mate = fold_ref[:, :1] - at
            mate = jnp.where(mate < 0, mate + lon_points, mate)
            mate = jnp.where(mate < 0, mate + lon_points, mate)
            mate = jnp.where(mate >= lon_points, mate - lon_points, mate)
            pick = jnp.where(point == mate, 1.0, 0.0).astype(BF16)
            for r in range(HALO):
                ext[rows + HALO + r] = jnp.dot(top_all[HALO - 1 - r], pick, preferred_element_type=F32)

    here = pl.ds(pl.multiple_of(lon * cols, LANES), cols)

    def row_at(chunk, q):
        return lax.rem(chunk * lon_n + q + HALO, rows)

    def send_row(chunk, k):
        s = chunk * (lon_n - 1) + lon_n - 1 - k
        return pltpu.make_async_remote_copy(
            res.at[row_at(chunk, target(k))], by_rows.at[chunk, :, here],
            out_send.at[s], out_recv.at[s], device_id={"lon": target(k)})

    def send_back(chunk, k):
        q = target(k)
        s = chunk * (lon_n - 1) + lon_n - 1 - k
        return pltpu.make_async_remote_copy(
            back.at[chunk, :, pl.ds(pl.multiple_of(q * cols, LANES), cols)], spatial.at[chunk * lon_n + lon],
            in_send.at[s], in_recv.at[s], device_id={"lon": q})

    inside = lax.broadcasted_iota(jnp.int32, (padded, 2 * cols), 0) < channels

    def mix_rows(chunk):
        @pl.loop(0, lon_n // 2)
        def _(pair):
            k = lon_n - 1 - 2 * pair
            one, two = row_at(chunk, target(k)), row_at(chunk, target(k - 1))
            x = jnp.concatenate([depth[one], depth[two]], axis=1)
            mean = jnp.sum(x, axis=0, keepdims=True) * (1.0 / channels)
            centred = jnp.where(inside, x - mean, 0.0)
            var = jnp.sum(centred * centred, axis=0, keepdims=True) * (1.0 / channels)
            normed = (centred * lax.rsqrt(var + 1e-06) * gain_col[:, :1]).astype(BF16)
            pre = jnp.dot(w_in_t[...], normed, preferred_element_type=F32)
            hidden = jax.nn.gelu(pre, approximate=True).astype(BF16)
            branch = jnp.dot(w_out_t[...], hidden, preferred_element_type=F32)
            for n, row in enumerate((one, two)):
                wet_row = mask_ref[pl.ds(row, 1), :].astype(F32)
                part = branch[:, n * cols : (n + 1) * cols]
                res[row] = (wet_row * (own[row].astype(F32) + part)).astype(BF16)
            send_row(chunk, k).start()

            @pl.when(pair < lon_n // 2 - 1)
            def _():
                send_row(chunk, k - 1).start()

            @pl.when(pair == lon_n // 2 - 1)
            def _():
                by_rows[chunk, :, here] = res[two]

    def spectral(chunk):
        for k in range(lon_n - 1, 0, -1):
            send_row(chunk, k).wait_recv()
        spectrum = jnp.dot(by_rows[chunk], table_ref[...], preferred_element_type=F32)
        s_re = spectrum[:channels, :modes]
        s_im = spectrum[:channels, modes:]
        g_re = spec_ref[0]
        g_im = spec_ref[1]
        scaled = jnp.concatenate(
            [(g_re * s_re - g_im * s_im).astype(BF16), (g_re * s_im + g_im * s_re).astype(BF16)], axis=1)
        back[chunk, :channels] = lax.dot_general(
            scaled, table_ref[...], (((1,), (1,)), ((), ())), preferred_element_type=F32).astype(BF16)
        for k in range(lon_n - 1, 0, -1):
            send_back(chunk, k).start()
        spatial[chunk * lon_n + lon] = back[chunk, :, here]

    def finish(chunk):
        @pl.loop(0, lon_n)
        def _(k):
            @pl.when(k > 0)
            def _():
                send_back(chunk, k).wait_recv()

            pos = source(k)
            row = row_at(chunk, pos)
            mixed = jnp.dot(mix_t[...], spatial[chunk * lon_n + pos], preferred_element_type=F32)
            wet_row = mask_ref[pl.ds(row, 1), :].astype(F32)
            val = wet_row * (res[row].astype(F32) + mixed)
            flat[0, pl.ds(row, padded, stride=rows), :] = val[:, :LANES]
            flat[1, pl.ds(row, padded, stride=rows), :] = val[:, LANES:]

    halo_done = False
    for chunk in range(per):
        out_rows = [(chunk * lon_n + q + HALO) % rows for q in range(lon_n)]
        if not halo_done and (min(out_rows) < HALO or max(out_rows) >= rows - HALO):
            await_halo()
            halo_done = True
        conv(out_rows)
        mix_rows(chunk)
        if chunk == 1:
            table_copy.wait()
            spec_copy.wait()
        if chunk >= 1:
            spectral(chunk - 1)
    if per == 1:
        table_copy.wait()
        spec_copy.wait()
    for chunk in range(per - 2):
        finish(chunk)
    spectral(per - 1)
    for chunk in range(max(per - 2, 0), per):
        finish(chunk)

    @pl.loop(0, channels)
    def _(c):
        at = pl.multiple_of(c * rows, rows)
        out_ref[c, :, :LANES] = flat[0, pl.ds(at, rows), :].astype(BF16)
        out_ref[c, :, LANES:] = flat[1, pl.ds(at, rows), :].astype(BF16)

    for chunk in range(per):
        for k in range(lon_n - 1, 0, -1):
            send_row(chunk, k).wait_send()
            send_back(chunk, k).wait_send()


def local(lat_n, lon_n, field, land_mask, fold_partner, dw_kernel, norm_gain, w_in, w_out, spec_gain, mix_weight):
    channels, rows, cols = field.shape
    modes = spec_gain.shape[2]
    hid = w_in.shape[1]
    lon_points = cols * lon_n
    padded = -(-channels // 16) * 16
    hid_up = -(-hid // 16) * 16
    table = jnp.asarray(dft_table(lon_points, modes))
    taps = dw_kernel.reshape(channels, -1)
    per = rows // lon_n
    sizes = (channels, padded, rows, cols, lat_n, lon_n, modes)
    vmem = pl.BlockSpec(memory_space=pltpu.VMEM)
    hbm = pl.BlockSpec(memory_space=pl.ANY)
    dma = pltpu.SemaphoreType.DMA
    peers = lon_n - 1
    return pl.pallas_call(
        functools.partial(kernel, sizes),
        out_shape=jax.ShapeDtypeStruct(field.shape, BF16),
        in_specs=[vmem] * 8 + [hbm] * 2,
        out_specs=vmem,
        scratch_shapes=[
            pltpu.VMEM((2, padded * rows, LANES), F32),
            pltpu.VMEM((rows + 2 * HALO, padded, cols + LANES), F32),
            pltpu.VMEM((rows, padded, cols), BF16),
            pltpu.VMEM((rows, padded, cols), F32),
            pltpu.VMEM((rows, padded, cols), BF16),
            pltpu.VMEM((per, padded, lon_points), BF16),
            pltpu.VMEM((per, padded, lon_points), BF16),
            pltpu.VMEM((rows, padded, cols), BF16),
            *[pltpu.VMEM((padded, LANES), BF16)] * 6,
            *[pltpu.VMEM((HALO, padded, cols), BF16)] * 2,
            pltpu.VMEM((HALO, padded, lon_points), BF16),
            pltpu.VMEM(spec_gain.shape, F32),
            pltpu.VMEM(table.shape, BF16),
            pltpu.VMEM((TAPS * TAPS, padded, LANES), F32),
            pltpu.VMEM((hid_up, padded), BF16),
            pltpu.VMEM((padded, hid_up), BF16),
            pltpu.VMEM((padded, padded), BF16),
            pltpu.VMEM((padded, LANES), F32),
            *[dma((2,))] * 7,
            *[dma((peers,))] * 2,
            *[dma((peers * per,))] * 4,
        ],
        compiler_params=pltpu.CompilerParams(
            collective_id=0, has_side_effects=True, vmem_limit_bytes=62 * 1024 * 1024),
        name="block",
    )(field, land_mask, fold_partner[None, :], taps, norm_gain[None, :], w_in, w_out, mix_weight, spec_gain, table)


def solution(mesh):
    placed = (P(None, "lat", "lon"), P("lat", "lon"), P(), P(), P(), P(), P(), P(), P())
    return jax.shard_map(
        functools.partial(local, mesh.shape["lat"], mesh.shape["lon"]),
        mesh=mesh, in_specs=placed, out_specs=P(None, "lat", "lon"), check_vma=False,
    )
```

time: 80.5 us -> 62.2 us (0.77); the launches traced: 79 us -> 61.9 us
  Pallas kernels: 65.8 us -> 54.1 us
  local copies, waits for them, and re-layouts: 11.9 us -> 7.8 us
  other arithmetic: 1.24 us -> 0 us
    pallas_call x1, Pallas kernels: 65.8 us -> 54.1 us  [local(): pl.pallas_call(functools.partial(kernel, sizes), out_shape=jax.ShapeDtype...]
    pad x6 -> x0, local copies, waits for them, and re-layouts: 5.27 us -> none  [the longest x1 1.63 us: local(): w_out_t = jnp.pad(w_out.T, ((0, extra), (0, hid_pad - hid)))]
    unnamed x8 -> x3, local copies, waits for them, and re-layouts: 3.68 us -> 6.25 us
    slice x1 -> x0, local copies, waits for them, and re-layouts: 1.27 us -> none  [local(): fold_partner[0] - (lax.axis_index('lon') * cols + column)]
    select_n x1 -> x0, other arithmetic: 1.24 us -> none  [local(): (fold_partner[0] - (lax.axis_index('lon') * cols + column)) % lon_points]
where the time goes in v2:
time: 62.2 us; the launch traced here: 61.9 us
  Pallas kernels  54.1 us (87%)
  local copies, waits for them, and re-layouts  7.8 us (13%)
    pallas_call x1, Pallas kernels, local(): pl.pallas_call(functools.partial(kernel, sizes), out_shape=jax.ShapeDtype...  54.1 us
    unnamed x3, local copies, waits for them, and re-layouts  6.25 us
    reshape x2, local copies, waits for them, and re-layouts, local(): taps = dw_kernel.reshape(channels, -1)  1.56 us

profile of v2, /device:TPU:0, one launch (start us, length us, event | category | flops | bytes accessed | tf_op | source)
XLA Modules:
  0.0 61.9 jit_solution(10380201588139866014)
XLA Ops:
  0.0 0.8 %reshape.3 = f32[150,49]{0,1:T(8,128)S(1)} reshape(f32[150,7,7]{0,2,1:T(8,128)} %param.13) | data formatting | bytes 58800 | tf_op jit(solution)/shard_map/reshape | solution.py:363
  0.8 0.7 %copy.14.taps_ref = f32[150,49]{1,0:T(8,128)} copy(f32[150,49]{0,1:T(8,128)S(1)} %reshape.3) | data formatting | bytes 58800 | tf_op jit(solution)/shard_map/reshape | solution.py:363
  1.6 1.8 %copy.15.w_out_ref = bf16[600,150]{1,0:T(8,128)(2,1)} copy(bf16[600,150]{0,1:T(8,128)(2,1)} %param.16) | data formatting | bytes 360000 | tf_op args[6]
  3.4 2.0 %copy.16.spec_hbm = f32[2,150,512]{2,1,0:T(8,128)} copy(f32[2,150,512]{2,0,1:T(2,128)} %param.17) | data formatting | bytes 1228800 | tf_op args[7]
  5.4 54.1 %block.1 = bf16[150,16,256]{2,1,0:T(8,128)(2,1)} custom-call(bf16[150,16,256]{2,1,0:T(8,128)(2,1)} %field_ref.1, s32[16,256]{1,0:T(8,128)} %mask_ref.1, s32[1,1024]{1,0:T(1,128)} %bitcast.4, f32[150,49]{1,0:T(8,128)} %copy.14.taps_ref, f32[1,150]{1,0:T(1,128)} %bitcast.5, bf16[150,600]{1,0:T(8,128)(2,1)} %w_in_ref.1, bf16[600,150]{1,0:T(8,128)(2,1)} %copy.15.w_out_ref, ...), custom_call_target="tpu_custom_call" | custom-call | tf_op jit(solution)/shard_map/block/pallas_call | solution.py:370
  59.5 2.4 %copy.18 = bf16[150,16,256]{2,1,0:T(8,128)(2,1)} copy(bf16[150,16,256]{2,1,0:T(8,128)(2,1)} %block.1) | data formatting | bytes 2457600

commit v3 on v2

--- a/solution.py
+++ b/solution.py
@@ -138,8 +138,12 @@
         top_all[:, :, pl.ds(pl.multiple_of(lon * cols, LANES), cols)] = own[rows - HALO :]
 
     wide_taps[:, padded - 16 :, :] = jnp.zeros((TAPS * TAPS, 16, LANES), F32)
-    for t in range(TAPS * TAPS):
-        wide_taps[t, :channels, :] = jnp.broadcast_to(taps_ref[:, t : t + 1], (channels, LANES))
+    chan_up = -(-channels // LANES) * LANES
+    for a in range(TAPS):
+        line = jnp.concatenate([taps_ref[a], jnp.zeros((TAPS, chan_up - channels), F32)], axis=1)
+        line = jnp.concatenate([line, jnp.zeros((LANES - TAPS, chan_up), F32)], axis=0).T
+        for b in range(TAPS):
+            wide_taps[a * TAPS + b, :channels, :] = jnp.broadcast_to(line[:channels, b : b + 1], (channels, LANES))
 
     def turned(ref, target_ref):
         n, m = ref.shape
@@ -149,7 +153,9 @@
         target_ref[...] = full.T[: target_ref.shape[0], : target_ref.shape[1]].astype(BF16)
 
     turned(w_in_ref, w_in_t)
-    turned(w_out_ref, w_out_t)
+    hid = w_out_ref.shape[1]
+    w_out_t[...] = jnp.zeros(w_out_t.shape, BF16)
+    w_out_t[:channels, :hid] = w_out_ref[...]
     turned(mix_ref, mix_t)
     diagonal = lax.broadcasted_iota(jnp.int32, (padded, channels), 0) == lax.broadcasted_iota(
         jnp.int32, (padded, channels), 1)
@@ -360,7 +366,7 @@
     padded = -(-channels // 16) * 16
     hid_up = -(-hid // 16) * 16
     table = jnp.asarray(dft_table(lon_points, modes))
-    taps = dw_kernel.reshape(channels, -1)
+    taps = dw_kernel.transpose(1, 2, 0)
     per = rows // lon_n
     sizes = (channels, padded, rows, cols, lat_n, lon_n, modes)
     vmem = pl.BlockSpec(memory_space=pltpu.VMEM)
@@ -398,7 +404,7 @@
         compiler_params=pltpu.CompilerParams(
             collective_id=0, has_side_effects=True, vmem_limit_bytes=62 * 1024 * 1024),
         name="block",
-    )(field, land_mask, fold_partner[None, :], taps, norm_gain[None, :], w_in, w_out, mix_weight, spec_gain, table)
+    )(field, land_mask, fold_partner[None, :], taps, norm_gain[None, :], w_in, w_out.T, mix_weight, spec_gain, table)
 
 
 def solution(mesh):

time: 62.2 us -> 58.7 us (0.944)
  local copies, waits for them, and re-layouts: 7.8 us -> 4.42 us
    unnamed x3 -> x2, local copies, waits for them, and re-layouts: 6.25 us -> 4.42 us
    reshape x2 -> x0, local copies, waits for them, and re-layouts: 1.56 us -> none  [local(): taps = dw_kernel.reshape(channels, -1)]
where the time goes in v3:
time: 58.7 us; the launch traced here: 58.5 us
  Pallas kernels  54.1 us (92%)
  local copies, waits for them, and re-layouts  4.42 us (8%)
    pallas_call x1, Pallas kernels, local(): pl.pallas_call(functools.partial(kernel, sizes), out_shape=jax.ShapeDtype...  54.1 us
    unnamed x2, local copies, waits for them, and re-layouts  4.42 us

profile of v3, /device:TPU:0, one launch (start us, length us, event | category | flops | bytes accessed | tf_op | source)
XLA Modules:
  0.0 58.5 jit_solution(9388470326375301727)
XLA Ops:
  0.0 2.0 %copy.11.spec_hbm = f32[2,150,512]{2,1,0:T(8,128)} copy(f32[2,150,512]{2,0,1:T(2,128)} %param.17) | data formatting | bytes 1228800 | tf_op args[7]
  2.0 54.1 %block.1 = bf16[150,16,256]{2,1,0:T(8,128)(2,1)} custom-call(bf16[150,16,256]{2,1,0:T(8,128)(2,1)} %field_ref.1, s32[16,256]{1,0:T(8,128)} %mask_ref.1, s32[1,1024]{1,0:T(1,128)} %bitcast.6, f32[7,7,150]{2,1,0:T(8,128)} %bitcast.5, f32[1,150]{1,0:T(1,128)} %bitcast.7, bf16[150,600]{1,0:T(8,128)(2,1)} %w_in_ref.1, bf16[150,600]{1,0:T(8,128)(2,1)} %bitcast.4, ...), custom_call_target="tpu_custom_call" | custom-call | tf_op jit(solution)/shard_map/block/pallas_call | solution.py:376
  56.1 2.4 %copy.13 = bf16[150,16,256]{2,1,0:T(8,128)(2,1)} copy(bf16[150,16,256]{2,1,0:T(8,128)(2,1)} %block.1) | data formatting | bytes 2457600
